TPU v7x, 32 devices: a whole 2x2x4 slice. The times are simulated.
32 devices in a mesh: srow: 4 (over y, core), scol: 8 (over z, x).
Axes of the slice: x: 2, y: 2, z: 4, core: 2. Of those that a mesh axis runs over, the one named last changes fastest.
Arguments:
- loads: float32 [4, 16, 4, 128], P('srow', 'scol'), may hold values from -6 to 6
- local_inverse: float32 [4, 16, 128, 128], P('srow', 'scol'), as said below
- dirichlet: float32 [4, 16, 128, 128], P('srow', 'scol'), as said below
- corner_coupling: float32 [4, 16, 128], P('srow', 'scol'), may hold values from -4 to 4
- coarse_inverse: float32 [4, 16, 16], P('srow', 'scol'), as said below
- partner: int32 [4, 16, 128], P('srow', 'scol'), may hold values from -1 to 31, as said below
Outputs:
- multipliers: float32 [4, 16, 4, 128], P('srow', 'scol')
- residual: float32 [4, 16, 4, 128], P('srow', 'scol')
Inputs may be any that keep to these rules, and one draw needn't show every extreme that they name: `partner`: on each edge of each subdomain the first n entries, for some n of 1 to 32, are the positions 0 to n - 1 in order or reversed, the rest are -1; the two subdomains sharing an edge have the same n and mutually inverse lists. `local_inverse`: each block is symmetric positive definite. `dirichlet`: each block is symmetric positive definite. `coarse_inverse`: each band's matrix is symmetric positive definite.
All inputs are finite; a program needn't handle non-finite values.
Results may differ from a plain program's by a relative error of at most 0.0003.
Values sent between devices are 32-bit elements; how exact they have to be, the bound alone decides.
A program may use at most 64 MiB of HBM per device.

v0:
```python
import jax
import jax.numpy as jnp
from jax import lax
from jax.sharding import PartitionSpec as P

ITERS = 3
precise = lax.Precision.HIGHEST


def with_halo(cells, sides, width):
    for axis, dim in sides:
        count = lax.axis_size(axis)
        head = lax.slice_in_dim(cells, 0, width, axis=dim)
        tail = lax.slice_in_dim(cells, cells.shape[dim] - width, cells.shape[dim], axis=dim)
        cells = jnp.concatenate(
            [
                lax.ppermute(tail, axis, [(i, (i + 1) % count) for i in range(count)]),
                cells,
                lax.ppermute(head, axis, [((i + 1) % count, i) for i in range(count)]),
            ],
            axis=dim,
        )
    return cells


def facing_edges(values):
    edge_len = values.shape[-1] // 4
    sideways = with_halo(values[..., 0 : 2 * edge_len], (("scol", 1),), 1)
    vertical = with_halo(values[..., 2 * edge_len :], (("srow", 0),), 1)
    west_side = sideways[:, :-2, :, edge_len : 2 * edge_len]
    east_side = sideways[:, 2:, :, 0:edge_len]
    south_side = vertical[:-2, :, :, edge_len : 2 * edge_len]
    north_side = vertical[2:, :, :, 0:edge_len]
    return jnp.concatenate([west_side, east_side, south_side, north_side], axis=-1)


def jump(values, partner):
    edge_len = values.shape[-1] // 4
    facing = facing_edges(values)
    offset = jnp.arange(values.shape[-1], dtype=jnp.int32) // edge_len * edge_len
    position = jnp.clip(partner, 0, edge_len - 1) + offset
    position = jnp.broadcast_to(position[:, :, None, :], values.shape)
    picked = jnp.take_along_axis(facing, position, axis=-1)
    return jnp.where(partner[:, :, None, :] >= 0, values - picked, jnp.zeros_like(values))


def apply_inverse(values, local_inverse, corner_coupling, coarse_inverse):
    sub_rows, sub_cols, rhs_count, width = values.shape
    blocks = jnp.einsum("ijab,ijrb->ijra", local_inverse, values, precision=precise)
    coarse_in = jnp.einsum("ijb,ijrb->ijr", corner_coupling, values, precision=precise)
    coarse_in = coarse_in.reshape(sub_rows * sub_cols, rhs_count)
    band_rows = coarse_inverse[0]
    coarse_out = jnp.dot(
        band_rows,
        lax.all_gather(coarse_in, "scol", axis=0, tiled=True),
        precision=precise,
        preferred_element_type=jnp.float32,
    )
    coarse_out = coarse_out.reshape(sub_rows, sub_cols, rhs_count)
    return blocks + corner_coupling[:, :, None, :] * coarse_out[..., None]


def inner(left, right):
    return jnp.sum(left * right, axis=(0, 1, 3))


def global_sums(first_dot, second_dot):
    return lax.psum((first_dot, second_dot), ("srow", "scol"))


def scaled(coef, values):
    return coef[None, None, :, None] * values


def body(loads, local_inverse, dirichlet, corner_coupling, coarse_inverse, partner):

    def operator(values):
        spread = jump(values, partner)
        return jump(apply_inverse(spread, local_inverse, corner_coupling, coarse_inverse), partner)

    def precond(values):
        spread = jump(values, partner)
        return jump(jnp.einsum("ijab,ijrb->ijra", dirichlet, spread, precision=precise), partner)

    right = operator(loads)
    multipliers = jnp.zeros_like(right)
    residual = right
    precon = precond(residual)
    image = operator(precon)
    gamma, curvature = global_sums(inner(residual, precon), inner(precon, image))
    step_size = gamma / curvature
    search = precon
    along = image
    for iteration in range(ITERS):
        multipliers = multipliers + scaled(step_size, search)
        residual = residual - scaled(step_size, along)
        if iteration + 1 < ITERS:
            precon = precond(residual)
            image = operator(precon)
            gamma_new, curvature = global_sums(inner(residual, precon), inner(precon, image))
            dir_ratio = gamma_new / gamma
            step_size = gamma_new / (curvature - dir_ratio * gamma_new / step_size)
            search = precon + scaled(dir_ratio, search)
            along = image + scaled(dir_ratio, along)
            gamma = gamma_new
    return (multipliers, residual)


def solution(mesh):
    return jax.shard_map(
        body,
        mesh=mesh,
        in_specs=(
            P("srow", "scol", None, None),
            P("srow", "scol", None, None),
            P("srow", "scol", None, None),
            P("srow", "scol", None),
            P("srow", "scol", None),
            P("srow", "scol", None),
        ),
        out_specs=(P("srow", "scol", None, None), P("srow", "scol", None, None)),
        check_vma=False,
    )
```

profile of v0, /device:TPU:0, one launch (start us, length us, event | category | flops | bytes accessed | tf_op | source)
XLA Modules:
  0.0 464.1 jit_solution(16173901481340105120)
XLA Ops:
  6.2 3.1 collective-permute-start.1
  10.9 9.6 %gather_fusion = f32[1024]{0:T(1024)S(1)} fusion(f32[2,4,128]{2,1,0:T(4,128)S(1)} %fusion.69, s32[1024]{0:T(1024)S(1)} %bitcast.196), kind=kCustom, calls=%fused_computation.clone | custom fusion | bytes 20480 | tf_op jit(solution)/shard_map/jit(take_along_axis)/gather | solution.py:43
  21.3 21.1 %all-gather = f32[8,2,4]{2,1,0:T(2,128)S(1)} all-gather(f32[1,2,4]{2,1,0:T(2,128)S(1)} %bitcast.256), channel_id=1, replica_groups=mesh['srow'=4,'scol'=8] {'scol'}, dimensions={0}, use_global_device_ids=true | all-gather | bytes 288 | tf_op jit(solution)/shard_map/all_gather | solution.py:55
  45.4 4.7 %collective-permute-start.5 = (f32[1,1,4,64]{3,2,1,0:T(4,128)S(1)}, f32[1,1,4,64]{3,2,1,0:T(4,128)S(1)}, u32[]{:S(2)}, u32[]{:S(2)}) collective-permute-start(f32[1,1,4,64]{3,2,1,0:T(4,128)S(1)} %get-tuple-element.76), channel_id=1, source_target_pairs={{1,0},{2,1},{3,2},{4,3},{5,4},{6,5},{7,6},{0,7},{9,8},{10,9},{11,1... | collective-permute-start | bytes 3080 | tf_op jit(solution)/shard_map/ppermute | solution.py:19
  51.7 9.6 %gather_fusion.1 = f32[1024]{0:T(1024)S(1)} fusion(f32[2,4,128]{2,1,0:T(4,128)S(1)} %fusion.65, s32[1024]{0:T(1024)S(1)} %bitcast.197), kind=kCustom, calls=%fused_computation.1.clone | custom fusion | bytes 20480 | tf_op jit(solution)/shard_map/jit(take_along_axis)/gather | solution.py:43
  63.2 4.7 %collective-permute-start.9 = (f32[1,1,4,64]{3,2,1,0:T(4,128)S(1)}, f32[1,1,4,64]{3,2,1,0:T(4,128)S(1)}, u32[]{:S(2)}, u32[]{:S(2)}) collective-permute-start(f32[1,1,4,64]{3,2,1,0:T(4,128)S(1)} %get-tuple-element.72), channel_id=1, source_target_pairs={{1,0},{2,1},{3,2},{4,3},{5,4},{6,5},{7,6},{0,7},{9,8},{10,9},{11,1... | collective-permute-start | bytes 3080 | tf_op jit(solution)/shard_map/ppermute | solution.py:19
  69.6 9.6 %gather_fusion.2 = f32[1024]{0:T(1024)S(1)} fusion(f32[2,4,128]{2,1,0:T(4,128)S(1)} %fusion.61, s32[1024]{0:T(1024)S(1)} %bitcast.198), kind=kCustom, calls=%fused_computation.2.clone | custom fusion | bytes 20480 | tf_op jit(solution)/shard_map/jit(take_along_axis)/gather | solution.py:43
  81.3 4.7 %collective-permute-start.13 = (f32[1,1,4,64]{3,2,1,0:T(4,128)S(1)}, f32[1,1,4,64]{3,2,1,0:T(4,128)S(1)}, u32[]{:S(2)}, u32[]{:S(2)}) collective-permute-start(f32[1,1,4,64]{3,2,1,0:T(4,128)S(1)} %get-tuple-element.68), channel_id=1, source_target_pairs={{1,0},{2,1},{3,2},{4,3},{5,4},{6,5},{7,6},{0,7},{9,8},{10,9},{11,1... | collective-permute-start | bytes 3080 | tf_op jit(solution)/shard_map/ppermute | solution.py:19
  87.7 9.6 %gather_fusion.3 = f32[1024]{0:T(1024)S(1)} fusion(f32[2,4,128]{2,1,0:T(4,128)S(1)} %fusion.57, s32[1024]{0:T(1024)S(1)} %bitcast.199), kind=kCustom, calls=%fused_computation.3.clone | custom fusion | bytes 20480 | tf_op jit(solution)/shard_map/jit(take_along_axis)/gather | solution.py:43
  99.2 4.7 %collective-permute-start.17 = (f32[1,1,4,64]{3,2,1,0:T(4,128)S(1)}, f32[1,1,4,64]{3,2,1,0:T(4,128)S(1)}, u32[]{:S(2)}, u32[]{:S(2)}) collective-permute-start(f32[1,1,4,64]{3,2,1,0:T(4,128)S(1)} %get-tuple-element.64), channel_id=1, source_target_pairs={{1,0},{2,1},{3,2},{4,3},{5,4},{6,5},{7,6},{0,7},{9,8},{10,9},{11,1... | collective-permute-start | bytes 3080 | tf_op jit(solution)/shard_map/ppermute | solution.py:19
  105.5 9.6 %gather_fusion.4 = f32[1024]{0:T(1024)S(1)} fusion(f32[2,4,128]{2,1,0:T(4,128)S(1)} %fusion.53, s32[1024]{0:T(1024)S(1)} %bitcast.200), kind=kCustom, calls=%fused_computation.4.clone | custom fusion | bytes 20480 | tf_op jit(solution)/shard_map/jit(take_along_axis)/gather | solution.py:43
  115.3 21.0 %all-gather.1 = f32[8,2,4]{2,1,0:T(2,128)S(1)} all-gather(f32[1,2,4]{2,1,0:T(2,128)S(1)} %bitcast.257), channel_id=1, replica_groups=mesh['srow'=4,'scol'=8] {'scol'}, dimensions={0}, use_global_device_ids=true | all-gather | bytes 288 | tf_op jit(solution)/shard_map/all_gather | solution.py:55
  138.6 4.7 %collective-permute-start.21 = (f32[1,1,4,64]{3,2,1,0:T(4,128)S(1)}, f32[1,1,4,64]{3,2,1,0:T(4,128)S(1)}, u32[]{:S(2)}, u32[]{:S(2)}) collective-permute-start(f32[1,1,4,64]{3,2,1,0:T(4,128)S(1)} %get-tuple-element.60), channel_id=1, source_target_pairs={{1,0},{2,1},{3,2},{4,3},{5,4},{6,5},{7,6},{0,7},{9,8},{10,9},{11,1... | collective-permute-start | bytes 3080 | tf_op jit(solution)/shard_map/ppermute | solution.py:19
  144.9 9.6 %gather_fusion.5 = f32[1024]{0:T(1024)S(1)} fusion(f32[2,4,128]{2,1,0:T(4,128)S(1)} %fusion.49, s32[1024]{0:T(1024)S(1)} %bitcast.201), kind=kCustom, calls=%fused_computation.5.clone | custom fusion | bytes 20480 | tf_op jit(solution)/shard_map/jit(take_along_axis)/gather | solution.py:43
  154.7 40.2 %all-reduce.2 = (f32[4]{0:T(128)S(1)}, f32[4]{0:T(128)S(1)}) all-reduce(f32[4]{0:T(128)S(1)} %get-tuple-element.8, f32[4]{0:T(128)S(1)} %get-tuple-element.7), channel_id=1, replica_groups=mesh['srow'=4,'scol'=8] {'srow','scol'}, use_global_device_ids=true, to_apply=%region_1.3 | all-reduce | flops 8 | bytes 64 | tf_op jit(solution)/shard_map/psum | solution.py:68
  203.2 9.6 %gather_fusion.6 = f32[1024]{0:T(1024)S(1)} fusion(f32[2,4,128]{2,1,0:T(4,128)S(1)} %fusion.45, s32[1024]{0:T(1024)S(1)} %bitcast.202), kind=kCustom, calls=%fused_computation.6.clone | custom fusion | bytes 20480 | tf_op jit(solution)/shard_map/jit(take_along_axis)/gather | solution.py:43
  216.7 2.9 collective-permute-start.29
  221.3 9.6 %gather_fusion.7 = f32[1024]{0:T(1024)S(1)} fusion(f32[2,4,128]{2,1,0:T(4,128)S(1)} %fusion.41, s32[1024]{0:T(1024)S(1)} %bitcast.203), kind=kCustom, calls=%fused_computation.7.clone | custom fusion | bytes 20480 | tf_op jit(solution)/shard_map/jit(take_along_axis)/gather | solution.py:43
  234.1 3.4 collective-permute-start.33
  239.1 9.6 %gather_fusion.8 = f32[1024]{0:T(1024)S(1)} fusion(f32[2,4,128]{2,1,0:T(4,128)S(1)} %fusion.37, s32[1024]{0:T(1024)S(1)} %bitcast.204), kind=kCustom, calls=%fused_computation.8.clone | custom fusion | bytes 20480 | tf_op jit(solution)/shard_map/jit(take_along_axis)/gather | solution.py:43
  248.9 21.0 %all-gather.2 = f32[8,2,4]{2,1,0:T(2,128)S(1)} all-gather(f32[1,2,4]{2,1,0:T(2,128)S(1)} %bitcast.258), channel_id=1, replica_groups=mesh['srow'=4,'scol'=8] {'scol'}, dimensions={0}, use_global_device_ids=true | all-gather | bytes 288 | tf_op jit(solution)/shard_map/all_gather | solution.py:55
  272.2 4.7 %collective-permute-start.37 = (f32[1,1,4,64]{3,2,1,0:T(4,128)S(1)}, f32[1,1,4,64]{3,2,1,0:T(4,128)S(1)}, u32[]{:S(2)}, u32[]{:S(2)}) collective-permute-start(f32[1,1,4,64]{3,2,1,0:T(4,128)S(1)} %get-tuple-element.44), channel_id=1, source_target_pairs={{1,0},{2,1},{3,2},{4,3},{5,4},{6,5},{7,6},{0,7},{9,8},{10,9},{11,1... | collective-permute-start | bytes 3080 | tf_op jit(solution)/shard_map/ppermute | solution.py:19
  278.5 9.6 %gather_fusion.9 = f32[1024]{0:T(1024)S(1)} fusion(f32[2,4,128]{2,1,0:T(4,128)S(1)} %fusion.33, s32[1024]{0:T(1024)S(1)} %bitcast.205), kind=kCustom, calls=%fused_computation.9.clone | custom fusion | bytes 20480 | tf_op jit(solution)/shard_map/jit(take_along_axis)/gather | solution.py:43
  288.3 40.8 %all-reduce.1 = (f32[4]{0:T(128)S(1)}, f32[4]{0:T(128)S(1)}) all-reduce(f32[4]{0:T(128)S(1)} %get-tuple-element.6, f32[4]{0:T(128)S(1)} %get-tuple-element.5), channel_id=1, replica_groups=mesh['srow'=4,'scol'=8] {'srow','scol'}, use_global_device_ids=true, to_apply=%region_5.7 | all-reduce | flops 8 | bytes 64 | tf_op jit(solution)/shard_map/psum | solution.py:68
  337.4 9.6 %gather_fusion.10 = f32[1024]{0:T(1024)S(1)} fusion(f32[2,4,128]{2,1,0:T(4,128)S(1)} %fusion.29, s32[1024]{0:T(1024)S(1)} %bitcast.206), kind=kCustom, calls=%fused_computation.10.clone | custom fusion | bytes 20480 | tf_op jit(solution)/shard_map/jit(take_along_axis)/gather | solution.py:43
  355.5 9.6 %gather_fusion.11 = f32[1024]{0:T(1024)S(1)} fusion(f32[2,4,128]{2,1,0:T(4,128)S(1)} %fusion.25, s32[1024]{0:T(1024)S(1)} %bitcast.207), kind=kCustom, calls=%fused_computation.11.clone | custom fusion | bytes 20480 | tf_op jit(solution)/shard_map/jit(take_along_axis)/gather | solution.py:43
  368.4 3.4 collective-permute-start.49
  373.4 9.6 %gather_fusion.12 = f32[1024]{0:T(1024)S(1)} fusion(f32[2,4,128]{2,1,0:T(4,128)S(1)} %fusion.21, s32[1024]{0:T(1024)S(1)} %bitcast.208), kind=kCustom, calls=%fused_computation.12.clone | custom fusion | bytes 20480 | tf_op jit(solution)/shard_map/jit(take_along_axis)/gather | solution.py:43
  383.1 21.0 %all-gather.3 = f32[8,2,4]{2,1,0:T(2,128)S(1)} all-gather(f32[1,2,4]{2,1,0:T(2,128)S(1)} %bitcast.259), channel_id=1, replica_groups=mesh['srow'=4,'scol'=8] {'scol'}, dimensions={0}, use_global_device_ids=true | all-gather | bytes 288 | tf_op jit(solution)/shard_map/all_gather | solution.py:55
  406.4 4.7 %collective-permute-start.53 = (f32[1,1,4,64]{3,2,1,0:T(4,128)S(1)}, f32[1,1,4,64]{3,2,1,0:T(4,128)S(1)}, u32[]{:S(2)}, u32[]{:S(2)}) collective-permute-start(f32[1,1,4,64]{3,2,1,0:T(4,128)S(1)} %get-tuple-element.28), channel_id=1, source_target_pairs={{1,0},{2,1},{3,2},{4,3},{5,4},{6,5},{7,6},{0,7},{9,8},{10,9},{11,1... | collective-permute-start | bytes 3080 | tf_op jit(solution)/shard_map/ppermute | solution.py:19
  412.8 9.6 %gather_fusion.13 = f32[1024]{0:T(1024)S(1)} fusion(f32[2,4,128]{2,1,0:T(4,128)S(1)} %fusion.17, s32[1024]{0:T(1024)S(1)} %bitcast.209), kind=kCustom, calls=%fused_computation.13.clone | custom fusion | bytes 20480 | tf_op jit(solution)/shard_map/jit(take_along_axis)/gather | solution.py:43
  422.5 40.8 %all-reduce = (f32[4]{0:T(128)S(1)}, f32[4]{0:T(128)S(1)}) all-reduce(f32[4]{0:T(128)S(1)} %get-tuple-element.4, f32[4]{0:T(128)S(1)} %get-tuple-element.3), channel_id=1, replica_groups=mesh['srow'=4,'scol'=8] {'srow','scol'}, use_global_device_ids=true, to_apply=%region_9.11 | all-reduce | flops 8 | bytes 64 | tf_op jit(solution)/shard_map/psum | solution.py:68
  (203 shorter events, 76.8 us)
Async XLA Ops:
  1.5 7.9 %collective-permute-start.2 = (f32[1,2,4,64]{3,2,1,0:T(4,128)S(1)}, f32[1,2,4,64]{3,2,1,0:T(4,128)S(1)}, u32[]{:S(2)}, u32[]{:S(2)}) collective-permute-start(f32[1,2,4,64]{3,2,1,0:T(4,128)S(1)} %get-tuple-element.77), channel_id=1, source_target_pairs={{0,8},{8,16},{16,24},{24,0},{1,9},{9,17},{17,25},{25,1},{2,10},{10... | collective-permute-start | bytes 6152 | tf_op jit(solution)/shard_map/ppermute | solution.py:17
  2.0 8.8 %collective-permute-start.3 = (f32[1,2,4,64]{3,2,1,0:T(4,128)S(1)}, f32[1,2,4,64]{3,2,1,0:T(4,128)S(1)}, u32[]{:S(2)}, u32[]{:S(2)}) collective-permute-start(f32[1,2,4,64]{3,2,1,0:T(4,128)S(1)} %get-tuple-element.77), channel_id=1, source_target_pairs={{8,0},{16,8},{24,16},{0,24},{9,1},{17,9},{25,17},{1,25},{10,2},{18... | collective-permute-start | bytes 6152 | tf_op jit(solution)/shard_map/ppermute | solution.py:19
  4.0 6.9 %collective-permute-start = (f32[1,1,4,64]{3,2,1,0:T(4,128)S(1)}, f32[1,1,4,64]{3,2,1,0:T(4,128)S(1)}, u32[]{:S(2)}, u32[]{:S(2)}) collective-permute-start(f32[1,1,4,64]{3,2,1,0:T(4,128)S(1)} %get-tuple-element.79), channel_id=1, source_target_pairs={{0,1},{1,2},{2,3},{3,4},{4,5},{5,6},{6,7},{7,0},{8,9},{9,10},{10,1... | collective-permute-start | bytes 3080 | tf_op jit(solution)/shard_map/ppermute | solution.py:17
  43.6 6.5 %collective-permute-start.6 = (f32[1,2,4,64]{3,2,1,0:T(4,128)S(1)}, f32[1,2,4,64]{3,2,1,0:T(4,128)S(1)}, u32[]{:S(2)}, u32[]{:S(2)}) collective-permute-start(f32[1,2,4,64]{3,2,1,0:T(4,128)S(1)} %get-tuple-element.73), channel_id=1, source_target_pairs={{0,8},{8,16},{16,24},{24,0},{1,9},{9,17},{17,25},{25,1},{2,10},{10... | collective-permute-start | bytes 6152 | tf_op jit(solution)/shard_map/ppermute | solution.py:17
  43.6 8.0 %collective-permute-start.7 = (f32[1,2,4,64]{3,2,1,0:T(4,128)S(1)}, f32[1,2,4,64]{3,2,1,0:T(4,128)S(1)}, u32[]{:S(2)}, u32[]{:S(2)}) collective-permute-start(f32[1,2,4,64]{3,2,1,0:T(4,128)S(1)} %get-tuple-element.73), channel_id=1, source_target_pairs={{8,0},{16,8},{24,16},{0,24},{9,1},{17,9},{25,17},{1,25},{10,2},{18... | collective-permute-start | bytes 6152 | tf_op jit(solution)/shard_map/ppermute | solution.py:19
  61.4 6.5 %collective-permute-start.10 = (f32[1,2,4,64]{3,2,1,0:T(4,128)S(1)}, f32[1,2,4,64]{3,2,1,0:T(4,128)S(1)}, u32[]{:S(2)}, u32[]{:S(2)}) collective-permute-start(f32[1,2,4,64]{3,2,1,0:T(4,128)S(1)} %get-tuple-element.69), channel_id=1, source_target_pairs={{0,8},{8,16},{16,24},{24,0},{1,9},{9,17},{17,25},{25,1},{2,10},{10... | collective-permute-start | bytes 6152 | tf_op jit(solution)/shard_map/ppermute | solution.py:17
  61.5 8.0 %collective-permute-start.11 = (f32[1,2,4,64]{3,2,1,0:T(4,128)S(1)}, f32[1,2,4,64]{3,2,1,0:T(4,128)S(1)}, u32[]{:S(2)}, u32[]{:S(2)}) collective-permute-start(f32[1,2,4,64]{3,2,1,0:T(4,128)S(1)} %get-tuple-element.69), channel_id=1, source_target_pairs={{8,0},{16,8},{24,16},{0,24},{9,1},{17,9},{25,17},{1,25},{10,2},{18... | collective-permute-start | bytes 6152 | tf_op jit(solution)/shard_map/ppermute | solution.py:19
  79.6 6.5 %collective-permute-start.14 = (f32[1,2,4,64]{3,2,1,0:T(4,128)S(1)}, f32[1,2,4,64]{3,2,1,0:T(4,128)S(1)}, u32[]{:S(2)}, u32[]{:S(2)}) collective-permute-start(f32[1,2,4,64]{3,2,1,0:T(4,128)S(1)} %get-tuple-element.65), channel_id=1, source_target_pairs={{0,8},{8,16},{16,24},{24,0},{1,9},{9,17},{17,25},{25,1},{2,10},{10... | collective-permute-start | bytes 6152 | tf_op jit(solution)/shard_map/ppermute | solution.py:17
  79.6 8.0 %collective-permute-start.15 = (f32[1,2,4,64]{3,2,1,0:T(4,128)S(1)}, f32[1,2,4,64]{3,2,1,0:T(4,128)S(1)}, u32[]{:S(2)}, u32[]{:S(2)}) collective-permute-start(f32[1,2,4,64]{3,2,1,0:T(4,128)S(1)} %get-tuple-element.65), channel_id=1, source_target_pairs={{8,0},{16,8},{24,16},{0,24},{9,1},{17,9},{25,17},{1,25},{10,2},{18... | collective-permute-start | bytes 6152 | tf_op jit(solution)/shard_map/ppermute | solution.py:19
  97.4 6.5 %collective-permute-start.18 = (f32[1,2,4,64]{3,2,1,0:T(4,128)S(1)}, f32[1,2,4,64]{3,2,1,0:T(4,128)S(1)}, u32[]{:S(2)}, u32[]{:S(2)}) collective-permute-start(f32[1,2,4,64]{3,2,1,0:T(4,128)S(1)} %get-tuple-element.61), channel_id=1, source_target_pairs={{0,8},{8,16},{16,24},{24,0},{1,9},{9,17},{17,25},{25,1},{2,10},{10... | collective-permute-start | bytes 6152 | tf_op jit(solution)/shard_map/ppermute | solution.py:17
  97.4 8.0 %collective-permute-start.19 = (f32[1,2,4,64]{3,2,1,0:T(4,128)S(1)}, f32[1,2,4,64]{3,2,1,0:T(4,128)S(1)}, u32[]{:S(2)}, u32[]{:S(2)}) collective-permute-start(f32[1,2,4,64]{3,2,1,0:T(4,128)S(1)} %get-tuple-element.61), channel_id=1, source_target_pairs={{8,0},{16,8},{24,16},{0,24},{9,1},{17,9},{25,17},{1,25},{10,2},{18... | collective-permute-start | bytes 6152 | tf_op jit(solution)/shard_map/ppermute | solution.py:19
  99.2 6.3 %collective-permute-start.16 = (f32[1,1,4,64]{3,2,1,0:T(4,128)S(1)}, f32[1,1,4,64]{3,2,1,0:T(4,128)S(1)}, u32[]{:S(2)}, u32[]{:S(2)}) collective-permute-start(f32[1,1,4,64]{3,2,1,0:T(4,128)S(1)} %get-tuple-element.63), channel_id=1, source_target_pairs={{0,1},{1,2},{2,3},{3,4},{4,5},{5,6},{6,7},{7,0},{8,9},{9,10},{10,1... | collective-permute-start | bytes 3080 | tf_op jit(solution)/shard_map/ppermute | solution.py:17
  136.8 6.5 %collective-permute-start.22 = (f32[1,2,4,64]{3,2,1,0:T(4,128)S(1)}, f32[1,2,4,64]{3,2,1,0:T(4,128)S(1)}, u32[]{:S(2)}, u32[]{:S(2)}) collective-permute-start(f32[1,2,4,64]{3,2,1,0:T(4,128)S(1)} %get-tuple-element.57), channel_id=1, source_target_pairs={{0,8},{8,16},{16,24},{24,0},{1,9},{9,17},{17,25},{25,1},{2,10},{10... | collective-permute-start | bytes 6152 | tf_op jit(solution)/shard_map/ppermute | solution.py:17
  136.8 8.0 %collective-permute-start.23 = (f32[1,2,4,64]{3,2,1,0:T(4,128)S(1)}, f32[1,2,4,64]{3,2,1,0:T(4,128)S(1)}, u32[]{:S(2)}, u32[]{:S(2)}) collective-permute-start(f32[1,2,4,64]{3,2,1,0:T(4,128)S(1)} %get-tuple-element.57), channel_id=1, source_target_pairs={{8,0},{16,8},{24,16},{0,24},{9,1},{17,9},{25,17},{1,25},{10,2},{18... | collective-permute-start | bytes 6152 | tf_op jit(solution)/shard_map/ppermute | solution.py:19
  138.6 6.3 %collective-permute-start.20 = (f32[1,1,4,64]{3,2,1,0:T(4,128)S(1)}, f32[1,1,4,64]{3,2,1,0:T(4,128)S(1)}, u32[]{:S(2)}, u32[]{:S(2)}) collective-permute-start(f32[1,1,4,64]{3,2,1,0:T(4,128)S(1)} %get-tuple-element.59), channel_id=1, source_target_pairs={{0,1},{1,2},{2,3},{3,4},{4,5},{5,6},{6,7},{7,0},{8,9},{9,10},{10,1... | collective-permute-start | bytes 3080 | tf_op jit(solution)/shard_map/ppermute | solution.py:17
  195.1 6.5 %collective-permute-start.26 = (f32[1,2,4,64]{3,2,1,0:T(4,128)S(1)}, f32[1,2,4,64]{3,2,1,0:T(4,128)S(1)}, u32[]{:S(2)}, u32[]{:S(2)}) collective-permute-start(f32[1,2,4,64]{3,2,1,0:T(4,128)S(1)} %get-tuple-element.53), channel_id=1, source_target_pairs={{0,8},{8,16},{16,24},{24,0},{1,9},{9,17},{17,25},{25,1},{2,10},{10... | collective-permute-start | bytes 6152 | tf_op jit(solution)/shard_map/ppermute | solution.py:17
  195.1 8.0 %collective-permute-start.27 = (f32[1,2,4,64]{3,2,1,0:T(4,128)S(1)}, f32[1,2,4,64]{3,2,1,0:T(4,128)S(1)}, u32[]{:S(2)}, u32[]{:S(2)}) collective-permute-start(f32[1,2,4,64]{3,2,1,0:T(4,128)S(1)} %get-tuple-element.53), channel_id=1, source_target_pairs={{8,0},{16,8},{24,16},{0,24},{9,1},{17,9},{25,17},{1,25},{10,2},{18... | collective-permute-start | bytes 6152 | tf_op jit(solution)/shard_map/ppermute | solution.py:19
  213.2 6.5 %collective-permute-start.30 = (f32[1,2,4,64]{3,2,1,0:T(4,128)S(1)}, f32[1,2,4,64]{3,2,1,0:T(4,128)S(1)}, u32[]{:S(2)}, u32[]{:S(2)}) collective-permute-start(f32[1,2,4,64]{3,2,1,0:T(4,128)S(1)} %get-tuple-element.49), channel_id=1, source_target_pairs={{0,8},{8,16},{16,24},{24,0},{1,9},{9,17},{17,25},{25,1},{2,10},{10... | collective-permute-start | bytes 6152 | tf_op jit(solution)/shard_map/ppermute | solution.py:17
  213.2 8.0 %collective-permute-start.31 = (f32[1,2,4,64]{3,2,1,0:T(4,128)S(1)}, f32[1,2,4,64]{3,2,1,0:T(4,128)S(1)}, u32[]{:S(2)}, u32[]{:S(2)}) collective-permute-start(f32[1,2,4,64]{3,2,1,0:T(4,128)S(1)} %get-tuple-element.49), channel_id=1, source_target_pairs={{8,0},{16,8},{24,16},{0,24},{9,1},{17,9},{25,17},{1,25},{10,2},{18... | collective-permute-start | bytes 6152 | tf_op jit(solution)/shard_map/ppermute | solution.py:19
  231.0 6.5 %collective-permute-start.34 = (f32[1,2,4,64]{3,2,1,0:T(4,128)S(1)}, f32[1,2,4,64]{3,2,1,0:T(4,128)S(1)}, u32[]{:S(2)}, u32[]{:S(2)}) collective-permute-start(f32[1,2,4,64]{3,2,1,0:T(4,128)S(1)} %get-tuple-element.45), channel_id=1, source_target_pairs={{0,8},{8,16},{16,24},{24,0},{1,9},{9,17},{17,25},{25,1},{2,10},{10... | collective-permute-start | bytes 6152 | tf_op jit(solution)/shard_map/ppermute | solution.py:17
  231.0 8.0 %collective-permute-start.35 = (f32[1,2,4,64]{3,2,1,0:T(4,128)S(1)}, f32[1,2,4,64]{3,2,1,0:T(4,128)S(1)}, u32[]{:S(2)}, u32[]{:S(2)}) collective-permute-start(f32[1,2,4,64]{3,2,1,0:T(4,128)S(1)} %get-tuple-element.45), channel_id=1, source_target_pairs={{8,0},{16,8},{24,16},{0,24},{9,1},{17,9},{25,17},{1,25},{10,2},{18... | collective-permute-start | bytes 6152 | tf_op jit(solution)/shard_map/ppermute | solution.py:19
  270.4 6.5 %collective-permute-start.38 = (f32[1,2,4,64]{3,2,1,0:T(4,128)S(1)}, f32[1,2,4,64]{3,2,1,0:T(4,128)S(1)}, u32[]{:S(2)}, u32[]{:S(2)}) collective-permute-start(f32[1,2,4,64]{3,2,1,0:T(4,128)S(1)} %get-tuple-element.41), channel_id=1, source_target_pairs={{0,8},{8,16},{16,24},{24,0},{1,9},{9,17},{17,25},{25,1},{2,10},{10... | collective-permute-start | bytes 6152 | tf_op jit(solution)/shard_map/ppermute | solution.py:17
  270.4 8.0 %collective-permute-start.39 = (f32[1,2,4,64]{3,2,1,0:T(4,128)S(1)}, f32[1,2,4,64]{3,2,1,0:T(4,128)S(1)}, u32[]{:S(2)}, u32[]{:S(2)}) collective-permute-start(f32[1,2,4,64]{3,2,1,0:T(4,128)S(1)} %get-tuple-element.41), channel_id=1, source_target_pairs={{8,0},{16,8},{24,16},{0,24},{9,1},{17,9},{25,17},{1,25},{10,2},{18... | collective-permute-start | bytes 6152 | tf_op jit(solution)/shard_map/ppermute | solution.py:19
  329.3 6.5 %collective-permute-start.42 = (f32[1,2,4,64]{3,2,1,0:T(4,128)S(1)}, f32[1,2,4,64]{3,2,1,0:T(4,128)S(1)}, u32[]{:S(2)}, u32[]{:S(2)}) collective-permute-start(f32[1,2,4,64]{3,2,1,0:T(4,128)S(1)} %get-tuple-element.37), channel_id=1, source_target_pairs={{0,8},{8,16},{16,24},{24,0},{1,9},{9,17},{17,25},{25,1},{2,10},{10... | collective-permute-start | bytes 6152 | tf_op jit(solution)/shard_map/ppermute | solution.py:17
  329.3 8.0 %collective-permute-start.43 = (f32[1,2,4,64]{3,2,1,0:T(4,128)S(1)}, f32[1,2,4,64]{3,2,1,0:T(4,128)S(1)}, u32[]{:S(2)}, u32[]{:S(2)}) collective-permute-start(f32[1,2,4,64]{3,2,1,0:T(4,128)S(1)} %get-tuple-element.37), channel_id=1, source_target_pairs={{8,0},{16,8},{24,16},{0,24},{9,1},{17,9},{25,17},{1,25},{10,2},{18... | collective-permute-start | bytes 6152 | tf_op jit(solution)/shard_map/ppermute | solution.py:19
  347.4 6.5 %collective-permute-start.46 = (f32[1,2,4,64]{3,2,1,0:T(4,128)S(1)}, f32[1,2,4,64]{3,2,1,0:T(4,128)S(1)}, u32[]{:S(2)}, u32[]{:S(2)}) collective-permute-start(f32[1,2,4,64]{3,2,1,0:T(4,128)S(1)} %get-tuple-element.33), channel_id=1, source_target_pairs={{0,8},{8,16},{16,24},{24,0},{1,9},{9,17},{17,25},{25,1},{2,10},{10... | collective-permute-start | bytes 6152 | tf_op jit(solution)/shard_map/ppermute | solution.py:17
  347.4 8.0 %collective-permute-start.47 = (f32[1,2,4,64]{3,2,1,0:T(4,128)S(1)}, f32[1,2,4,64]{3,2,1,0:T(4,128)S(1)}, u32[]{:S(2)}, u32[]{:S(2)}) collective-permute-start(f32[1,2,4,64]{3,2,1,0:T(4,128)S(1)} %get-tuple-element.33), channel_id=1, source_target_pairs={{8,0},{16,8},{24,16},{0,24},{9,1},{17,9},{25,17},{1,25},{10,2},{18... | collective-permute-start | bytes 6152 | tf_op jit(solution)/shard_map/ppermute | solution.py:19
  365.2 6.5 %collective-permute-start.50 = (f32[1,2,4,64]{3,2,1,0:T(4,128)S(1)}, f32[1,2,4,64]{3,2,1,0:T(4,128)S(1)}, u32[]{:S(2)}, u32[]{:S(2)}) collective-permute-start(f32[1,2,4,64]{3,2,1,0:T(4,128)S(1)} %get-tuple-element.29), channel_id=1, source_target_pairs={{0,8},{8,16},{16,24},{24,0},{1,9},{9,17},{17,25},{25,1},{2,10},{10... | collective-permute-start | bytes 6152 | tf_op jit(solution)/shard_map/ppermute | solution.py:17
  365.3 8.0 %collective-permute-start.51 = (f32[1,2,4,64]{3,2,1,0:T(4,128)S(1)}, f32[1,2,4,64]{3,2,1,0:T(4,128)S(1)}, u32[]{:S(2)}, u32[]{:S(2)}) collective-permute-start(f32[1,2,4,64]{3,2,1,0:T(4,128)S(1)} %get-tuple-element.29), channel_id=1, source_target_pairs={{8,0},{16,8},{24,16},{0,24},{9,1},{17,9},{25,17},{1,25},{10,2},{18... | collective-permute-start | bytes 6152 | tf_op jit(solution)/shard_map/ppermute | solution.py:19
  367.0 6.3 %collective-permute-start.48 = (f32[1,1,4,64]{3,2,1,0:T(4,128)S(1)}, f32[1,1,4,64]{3,2,1,0:T(4,128)S(1)}, u32[]{:S(2)}, u32[]{:S(2)}) collective-permute-start(f32[1,1,4,64]{3,2,1,0:T(4,128)S(1)} %get-tuple-element.31), channel_id=1, source_target_pairs={{0,1},{1,2},{2,3},{3,4},{4,5},{5,6},{6,7},{7,0},{8,9},{9,10},{10,1... | collective-permute-start | bytes 3080 | tf_op jit(solution)/shard_map/ppermute | solution.py:17
  404.6 6.5 %collective-permute-start.54 = (f32[1,2,4,64]{3,2,1,0:T(4,128)S(1)}, f32[1,2,4,64]{3,2,1,0:T(4,128)S(1)}, u32[]{:S(2)}, u32[]{:S(2)}) collective-permute-start(f32[1,2,4,64]{3,2,1,0:T(4,128)S(1)} %get-tuple-element.25), channel_id=1, source_target_pairs={{0,8},{8,16},{16,24},{24,0},{1,9},{9,17},{17,25},{25,1},{2,10},{10... | collective-permute-start | bytes 6152 | tf_op jit(solution)/shard_map/ppermute | solution.py:17
  404.7 8.0 %collective-permute-start.55 = (f32[1,2,4,64]{3,2,1,0:T(4,128)S(1)}, f32[1,2,4,64]{3,2,1,0:T(4,128)S(1)}, u32[]{:S(2)}, u32[]{:S(2)}) collective-permute-start(f32[1,2,4,64]{3,2,1,0:T(4,128)S(1)} %get-tuple-element.25), channel_id=1, source_target_pairs={{8,0},{16,8},{24,16},{0,24},{9,1},{17,9},{25,17},{1,25},{10,2},{18... | collective-permute-start | bytes 6152 | tf_op jit(solution)/shard_map/ppermute | solution.py:19
  (30 other events, 198.2 us)
where the time goes:
time: 465 us; the launch traced here: 464 us
  blocking collectives  206 us (44%)
  local copies, waits for them, and re-layouts  139 us (30%)
  starting transfers between devices  92 us (20%)
  waiting for transfers between devices  20.7 us (4%)
    gather x14, local copies, waits for them, and re-layouts, jump(): picked = jnp.take_along_axis(facing, position, axis=-1)  134 us
    psum x3, blocking collectives, global_sums(): return lax.psum((first_dot, second_dot), ('srow', 'scol'))  122 us
    all_gather x4, blocking collectives, apply_inverse(): lax.all_gather(coarse_in, 'scol', axis=0, tiled=True)  84.1 us
    ppermute x28, starting transfers between devices, with_halo(): lax.ppermute(head, axis, [((i + 1) % count, i) for i in range(count)])  78.3 us
    ppermute x28, waiting for transfers between devices, with_halo(): lax.ppermute(tail, axis, [(i, (i + 1) % count) for i in range(count)])  20.7 us
    ppermute x28, starting transfers between devices, with_halo(): lax.ppermute(tail, axis, [(i, (i + 1) % count) for i in range(count)])  13.7 us
  transfers between devices with their start and end apart: 56, of which 14 were waited for; matrix products, arithmetic and copies ran while one was open for 0% of the time, Pallas kernels for 0%

commit v1 on v0

--- a/solution.py
+++ b/solution.py
@@ -65,7 +65,13 @@
 
 
 def global_sums(first_dot, second_dot):
-    return lax.psum((first_dot, second_dot), ("srow", "scol"))
+
+    def handle_case_on_mesh(xin):
+        for p in ("scol", "srow"):
+            xin = lax.psum(xin, p)
+        return xin
+
+    return handle_case_on_mesh((first_dot, second_dot))
 
 
 def scaled(coef, values):

time: 465 us -> 425 us (0.914)
  blocking collectives: 206 us -> 167 us
    psum x3 -> x6, blocking collectives: 122 us -> 82.5 us  [handle_case_on_mesh(): xin = lax.psum(xin, p)]
    ppermute x28, starting transfers between devices: 13.7 us -> 2.88 us  [with_halo(): lax.ppermute(tail, axis, [(i, (i + 1) % count) for i in range(count)])]
    ppermute x28, starting transfers between devices: 78.3 us -> 89.1 us  [with_halo(): lax.ppermute(head, axis, [((i + 1) % count, i) for i in range(count)])]
where the time goes in v1:
time: 425 us
  blocking collectives  167 us (39%)
  local copies, waits for them, and re-layouts  139 us (33%)
  starting transfers between devices  92 us (22%)
  waiting for transfers between devices  20.7 us (5%)
    gather x14, local copies, waits for them, and re-layouts, jump(): picked = jnp.take_along_axis(facing, position, axis=-1)  134 us
    ppermute x28, starting transfers between devices, with_halo(): lax.ppermute(head, axis, [((i + 1) % count, i) for i in range(count)])  89.1 us
    all_gather x4, blocking collectives, apply_inverse(): lax.all_gather(coarse_in, 'scol', axis=0, tiled=True)  84.1 us
    psum x6, blocking collectives, handle_case_on_mesh(): xin = lax.psum(xin, p)  82.5 us
    ppermute x28, waiting for transfers between devices, with_halo(): lax.ppermute(tail, axis, [(i, (i + 1) % count) for i in range(count)])  20.7 us
  transfers between devices with their start and end apart: 56, of which 14 were waited for; matrix products, arithmetic and copies ran while one was open for 0% of the time, Pallas kernels for 0%

profile of v1, /device:TPU:0, one launch (start us, length us, event | category | flops | bytes accessed | tf_op | source)
XLA Modules:
  0.0 424.6 jit_solution(13561833450493190565)
XLA Ops:
  10.9 9.6 %gather_fusion = f32[1024]{0:T(1024)S(1)} fusion(f32[2,4,128]{2,1,0:T(4,128)S(1)} %fusion.69, s32[1024]{0:T(1024)S(1)} %bitcast.196), kind=kCustom, calls=%fused_computation.clone | custom fusion | bytes 20480 | tf_op jit(solution)/shard_map/jit(take_along_axis)/gather | solution.py:43
  21.3 21.1 %all-gather = f32[8,2,4]{2,1,0:T(2,128)S(1)} all-gather(f32[1,2,4]{2,1,0:T(2,128)S(1)} %bitcast.256), channel_id=1, replica_groups=mesh['srow'=4,'scol'=8] {'scol'}, dimensions={0}, use_global_device_ids=true | all-gather | bytes 288 | tf_op jit(solution)/shard_map/all_gather | solution.py:55
  45.4 4.7 %collective-permute-start.5 = (f32[1,1,4,64]{3,2,1,0:T(4,128)S(1)}, f32[1,1,4,64]{3,2,1,0:T(4,128)S(1)}, u32[]{:S(2)}, u32[]{:S(2)}) collective-permute-start(f32[1,1,4,64]{3,2,1,0:T(4,128)S(1)} %get-tuple-element.82), channel_id=1, source_target_pairs={{1,0},{2,1},{3,2},{4,3},{5,4},{6,5},{7,6},{0,7},{9,8},{10,9},{11,1... | collective-permute-start | bytes 3080 | tf_op jit(solution)/shard_map/ppermute | solution.py:19
  51.7 9.6 %gather_fusion.1 = f32[1024]{0:T(1024)S(1)} fusion(f32[2,4,128]{2,1,0:T(4,128)S(1)} %fusion.65, s32[1024]{0:T(1024)S(1)} %bitcast.197), kind=kCustom, calls=%fused_computation.1.clone | custom fusion | bytes 20480 | tf_op jit(solution)/shard_map/jit(take_along_axis)/gather | solution.py:43
  63.2 4.7 %collective-permute-start.9 = (f32[1,1,4,64]{3,2,1,0:T(4,128)S(1)}, f32[1,1,4,64]{3,2,1,0:T(4,128)S(1)}, u32[]{:S(2)}, u32[]{:S(2)}) collective-permute-start(f32[1,1,4,64]{3,2,1,0:T(4,128)S(1)} %get-tuple-element.78), channel_id=1, source_target_pairs={{1,0},{2,1},{3,2},{4,3},{5,4},{6,5},{7,6},{0,7},{9,8},{10,9},{11,1... | collective-permute-start | bytes 3080 | tf_op jit(solution)/shard_map/ppermute | solution.py:19
  69.6 9.6 %gather_fusion.2 = f32[1024]{0:T(1024)S(1)} fusion(f32[2,4,128]{2,1,0:T(4,128)S(1)} %fusion.61, s32[1024]{0:T(1024)S(1)} %bitcast.198), kind=kCustom, calls=%fused_computation.2.clone | custom fusion | bytes 20480 | tf_op jit(solution)/shard_map/jit(take_along_axis)/gather | solution.py:43
  81.3 4.7 %collective-permute-start.13 = (f32[1,1,4,64]{3,2,1,0:T(4,128)S(1)}, f32[1,1,4,64]{3,2,1,0:T(4,128)S(1)}, u32[]{:S(2)}, u32[]{:S(2)}) collective-permute-start(f32[1,1,4,64]{3,2,1,0:T(4,128)S(1)} %get-tuple-element.74), channel_id=1, source_target_pairs={{1,0},{2,1},{3,2},{4,3},{5,4},{6,5},{7,6},{0,7},{9,8},{10,9},{11,1... | collective-permute-start | bytes 3080 | tf_op jit(solution)/shard_map/ppermute | solution.py:19
  87.7 9.6 %gather_fusion.3 = f32[1024]{0:T(1024)S(1)} fusion(f32[2,4,128]{2,1,0:T(4,128)S(1)} %fusion.57, s32[1024]{0:T(1024)S(1)} %bitcast.199), kind=kCustom, calls=%fused_computation.3.clone | custom fusion | bytes 20480 | tf_op jit(solution)/shard_map/jit(take_along_axis)/gather | solution.py:43
  99.2 4.7 %collective-permute-start.17 = (f32[1,1,4,64]{3,2,1,0:T(4,128)S(1)}, f32[1,1,4,64]{3,2,1,0:T(4,128)S(1)}, u32[]{:S(2)}, u32[]{:S(2)}) collective-permute-start(f32[1,1,4,64]{3,2,1,0:T(4,128)S(1)} %get-tuple-element.70), channel_id=1, source_target_pairs={{1,0},{2,1},{3,2},{4,3},{5,4},{6,5},{7,6},{0,7},{9,8},{10,9},{11,1... | collective-permute-start | bytes 3080 | tf_op jit(solution)/shard_map/ppermute | solution.py:19
  105.5 9.6 %gather_fusion.4 = f32[1024]{0:T(1024)S(1)} fusion(f32[2,4,128]{2,1,0:T(4,128)S(1)} %fusion.53, s32[1024]{0:T(1024)S(1)} %bitcast.200), kind=kCustom, calls=%fused_computation.4.clone | custom fusion | bytes 20480 | tf_op jit(solution)/shard_map/jit(take_along_axis)/gather | solution.py:43
  115.3 21.0 %all-gather.1 = f32[8,2,4]{2,1,0:T(2,128)S(1)} all-gather(f32[1,2,4]{2,1,0:T(2,128)S(1)} %bitcast.257), channel_id=1, replica_groups=mesh['srow'=4,'scol'=8] {'scol'}, dimensions={0}, use_global_device_ids=true | all-gather | bytes 288 | tf_op jit(solution)/shard_map/all_gather | solution.py:55
  138.6 4.7 %collective-permute-start.21 = (f32[1,1,4,64]{3,2,1,0:T(4,128)S(1)}, f32[1,1,4,64]{3,2,1,0:T(4,128)S(1)}, u32[]{:S(2)}, u32[]{:S(2)}) collective-permute-start(f32[1,1,4,64]{3,2,1,0:T(4,128)S(1)} %get-tuple-element.66), channel_id=1, source_target_pairs={{1,0},{2,1},{3,2},{4,3},{5,4},{6,5},{7,6},{0,7},{9,8},{10,9},{11,1... | collective-permute-start | bytes 3080 | tf_op jit(solution)/shard_map/ppermute | solution.py:19
  144.9 9.6 %gather_fusion.5 = f32[1024]{0:T(1024)S(1)} fusion(f32[2,4,128]{2,1,0:T(4,128)S(1)} %fusion.49, s32[1024]{0:T(1024)S(1)} %bitcast.201), kind=kCustom, calls=%fused_computation.5.clone | custom fusion | bytes 20480 | tf_op jit(solution)/shard_map/jit(take_along_axis)/gather | solution.py:43
  154.7 21.8 %all-reduce.2 = (f32[4]{0:T(128)S(1)}, f32[4]{0:T(128)S(1)}) all-reduce(f32[4]{0:T(128)S(1)} %get-tuple-element.8, f32[4]{0:T(128)S(1)} %get-tuple-element.7), channel_id=1, replica_groups=mesh['srow'=4,'scol'=8] {'scol'}, use_global_device_ids=true, to_apply=%region_1.3 | all-reduce | flops 8 | bytes 64 | tf_op jit(solution)/shard_map/psum | solution.py:71
  176.5 5.6 %all-reduce.5 = (f32[4]{0:T(128)S(1)}, f32[4]{0:T(128)S(1)}) all-reduce(f32[4]{0:T(128)S(1)} %get-tuple-element.13, f32[4]{0:T(128)S(1)} %get-tuple-element.14), channel_id=1, replica_groups=mesh['srow'=4,'scol'=8] {'srow'}, use_global_device_ids=true, to_apply=%region_2.4 | all-reduce | flops 8 | bytes 64 | tf_op jit(solution)/shard_map/psum | solution.py:71
  184.1 4.7 %collective-permute-start.25 = (f32[1,1,4,64]{3,2,1,0:T(4,128)S(1)}, f32[1,1,4,64]{3,2,1,0:T(4,128)S(1)}, u32[]{:S(2)}, u32[]{:S(2)}) collective-permute-start(f32[1,1,4,64]{3,2,1,0:T(4,128)S(1)} %get-tuple-element.62), channel_id=1, source_target_pairs={{1,0},{2,1},{3,2},{4,3},{5,4},{6,5},{7,6},{0,7},{9,8},{10,9},{11,1... | collective-permute-start | bytes 3080 | tf_op jit(solution)/shard_map/ppermute | solution.py:19
  190.5 9.6 %gather_fusion.6 = f32[1024]{0:T(1024)S(1)} fusion(f32[2,4,128]{2,1,0:T(4,128)S(1)} %fusion.45, s32[1024]{0:T(1024)S(1)} %bitcast.202), kind=kCustom, calls=%fused_computation.6.clone | custom fusion | bytes 20480 | tf_op jit(solution)/shard_map/jit(take_along_axis)/gather | solution.py:43
  202.2 4.7 %collective-permute-start.29 = (f32[1,1,4,64]{3,2,1,0:T(4,128)S(1)}, f32[1,1,4,64]{3,2,1,0:T(4,128)S(1)}, u32[]{:S(2)}, u32[]{:S(2)}) collective-permute-start(f32[1,1,4,64]{3,2,1,0:T(4,128)S(1)} %get-tuple-element.58), channel_id=1, source_target_pairs={{1,0},{2,1},{3,2},{4,3},{5,4},{6,5},{7,6},{0,7},{9,8},{10,9},{11,1... | collective-permute-start | bytes 3080 | tf_op jit(solution)/shard_map/ppermute | solution.py:19
  208.6 9.6 %gather_fusion.7 = f32[1024]{0:T(1024)S(1)} fusion(f32[2,4,128]{2,1,0:T(4,128)S(1)} %fusion.41, s32[1024]{0:T(1024)S(1)} %bitcast.203), kind=kCustom, calls=%fused_computation.7.clone | custom fusion | bytes 20480 | tf_op jit(solution)/shard_map/jit(take_along_axis)/gather | solution.py:43
  226.4 9.6 %gather_fusion.8 = f32[1024]{0:T(1024)S(1)} fusion(f32[2,4,128]{2,1,0:T(4,128)S(1)} %fusion.37, s32[1024]{0:T(1024)S(1)} %bitcast.204), kind=kCustom, calls=%fused_computation.8.clone | custom fusion | bytes 20480 | tf_op jit(solution)/shard_map/jit(take_along_axis)/gather | solution.py:43
  236.2 21.0 %all-gather.2 = f32[8,2,4]{2,1,0:T(2,128)S(1)} all-gather(f32[1,2,4]{2,1,0:T(2,128)S(1)} %bitcast.258), channel_id=1, replica_groups=mesh['srow'=4,'scol'=8] {'scol'}, dimensions={0}, use_global_device_ids=true | all-gather | bytes 288 | tf_op jit(solution)/shard_map/all_gather | solution.py:55
  259.4 4.7 %collective-permute-start.37 = (f32[1,1,4,64]{3,2,1,0:T(4,128)S(1)}, f32[1,1,4,64]{3,2,1,0:T(4,128)S(1)}, u32[]{:S(2)}, u32[]{:S(2)}) collective-permute-start(f32[1,1,4,64]{3,2,1,0:T(4,128)S(1)} %get-tuple-element.50), channel_id=1, source_target_pairs={{1,0},{2,1},{3,2},{4,3},{5,4},{6,5},{7,6},{0,7},{9,8},{10,9},{11,1... | collective-permute-start | bytes 3080 | tf_op jit(solution)/shard_map/ppermute | solution.py:19
  265.8 9.6 %gather_fusion.9 = f32[1024]{0:T(1024)S(1)} fusion(f32[2,4,128]{2,1,0:T(4,128)S(1)} %fusion.33, s32[1024]{0:T(1024)S(1)} %bitcast.205), kind=kCustom, calls=%fused_computation.9.clone | custom fusion | bytes 20480 | tf_op jit(solution)/shard_map/jit(take_along_axis)/gather | solution.py:43
  275.6 21.8 %all-reduce.1 = (f32[4]{0:T(128)S(1)}, f32[4]{0:T(128)S(1)}) all-reduce(f32[4]{0:T(128)S(1)} %get-tuple-element.6, f32[4]{0:T(128)S(1)} %get-tuple-element.5), channel_id=1, replica_groups=mesh['srow'=4,'scol'=8] {'scol'}, use_global_device_ids=true, to_apply=%region_7.9 | all-reduce | flops 8 | bytes 64 | tf_op jit(solution)/shard_map/psum | solution.py:71
  297.4 5.6 %all-reduce.4 = (f32[4]{0:T(128)S(1)}, f32[4]{0:T(128)S(1)}) all-reduce(f32[4]{0:T(128)S(1)} %get-tuple-element.11, f32[4]{0:T(128)S(1)} %get-tuple-element.12), channel_id=1, replica_groups=mesh['srow'=4,'scol'=8] {'srow'}, use_global_device_ids=true, to_apply=%region_8.10 | all-reduce | flops 8 | bytes 64 | tf_op jit(solution)/shard_map/psum | solution.py:71
  311.4 9.6 %gather_fusion.10 = f32[1024]{0:T(1024)S(1)} fusion(f32[2,4,128]{2,1,0:T(4,128)S(1)} %fusion.29, s32[1024]{0:T(1024)S(1)} %bitcast.206), kind=kCustom, calls=%fused_computation.10.clone | custom fusion | bytes 20480 | tf_op jit(solution)/shard_map/jit(take_along_axis)/gather | solution.py:43
  329.5 9.6 %gather_fusion.11 = f32[1024]{0:T(1024)S(1)} fusion(f32[2,4,128]{2,1,0:T(4,128)S(1)} %fusion.25, s32[1024]{0:T(1024)S(1)} %bitcast.207), kind=kCustom, calls=%fused_computation.11.clone | custom fusion | bytes 20480 | tf_op jit(solution)/shard_map/jit(take_along_axis)/gather | solution.py:43
  347.3 9.6 %gather_fusion.12 = f32[1024]{0:T(1024)S(1)} fusion(f32[2,4,128]{2,1,0:T(4,128)S(1)} %fusion.21, s32[1024]{0:T(1024)S(1)} %bitcast.208), kind=kCustom, calls=%fused_computation.12.clone | custom fusion | bytes 20480 | tf_op jit(solution)/shard_map/jit(take_along_axis)/gather | solution.py:43
  357.0 21.0 %all-gather.3 = f32[8,2,4]{2,1,0:T(2,128)S(1)} all-gather(f32[1,2,4]{2,1,0:T(2,128)S(1)} %bitcast.259), channel_id=1, replica_groups=mesh['srow'=4,'scol'=8] {'scol'}, dimensions={0}, use_global_device_ids=true | all-gather | bytes 288 | tf_op jit(solution)/shard_map/all_gather | solution.py:55
  386.7 9.6 %gather_fusion.13 = f32[1024]{0:T(1024)S(1)} fusion(f32[2,4,128]{2,1,0:T(4,128)S(1)} %fusion.17, s32[1024]{0:T(1024)S(1)} %bitcast.209), kind=kCustom, calls=%fused_computation.13.clone | custom fusion | bytes 20480 | tf_op jit(solution)/shard_map/jit(take_along_axis)/gather | solution.py:43
  396.5 21.8 %all-reduce = (f32[4]{0:T(128)S(1)}, f32[4]{0:T(128)S(1)}) all-reduce(f32[4]{0:T(128)S(1)} %get-tuple-element.4, f32[4]{0:T(128)S(1)} %get-tuple-element.3), channel_id=1, replica_groups=mesh['srow'=4,'scol'=8] {'scol'}, use_global_device_ids=true, to_apply=%region_13.15 | all-reduce | flops 8 | bytes 64 | tf_op jit(solution)/shard_map/psum | solution.py:71
  418.3 5.6 %all-reduce.3 = (f32[4]{0:T(128)S(1)}, f32[4]{0:T(128)S(1)}) all-reduce(f32[4]{0:T(128)S(1)} %get-tuple-element.9, f32[4]{0:T(128)S(1)} %get-tuple-element.10), channel_id=1, replica_groups=mesh['srow'=4,'scol'=8] {'srow'}, use_global_device_ids=true, to_apply=%region_14.16 | all-reduce | flops 8 | bytes 64 | tf_op jit(solution)/shard_map/psum | solution.py:71
  (206 shorter events, 84.9 us)
Async XLA Ops:
  1.5 7.9 %collective-permute-start.2 = (f32[1,2,4,64]{3,2,1,0:T(4,128)S(1)}, f32[1,2,4,64]{3,2,1,0:T(4,128)S(1)}, u32[]{:S(2)}, u32[]{:S(2)}) collective-permute-start(f32[1,2,4,64]{3,2,1,0:T(4,128)S(1)} %get-tuple-element.83), channel_id=1, source_target_pairs={{0,8},{8,16},{16,24},{24,0},{1,9},{9,17},{17,25},{25,1},{2,10},{10... | collective-permute-start | bytes 6152 | tf_op jit(solution)/shard_map/ppermute | solution.py:17
  2.0 8.8 %collective-permute-start.3 = (f32[1,2,4,64]{3,2,1,0:T(4,128)S(1)}, f32[1,2,4,64]{3,2,1,0:T(4,128)S(1)}, u32[]{:S(2)}, u32[]{:S(2)}) collective-permute-start(f32[1,2,4,64]{3,2,1,0:T(4,128)S(1)} %get-tuple-element.83), channel_id=1, source_target_pairs={{8,0},{16,8},{24,16},{0,24},{9,1},{17,9},{25,17},{1,25},{10,2},{18... | collective-permute-start | bytes 6152 | tf_op jit(solution)/shard_map/ppermute | solution.py:19
  4.0 6.9 %collective-permute-start = (f32[1,1,4,64]{3,2,1,0:T(4,128)S(1)}, f32[1,1,4,64]{3,2,1,0:T(4,128)S(1)}, u32[]{:S(2)}, u32[]{:S(2)}) collective-permute-start(f32[1,1,4,64]{3,2,1,0:T(4,128)S(1)} %get-tuple-element.85), channel_id=1, source_target_pairs={{0,1},{1,2},{2,3},{3,4},{4,5},{5,6},{6,7},{7,0},{8,9},{9,10},{10,1... | collective-permute-start | bytes 3080 | tf_op jit(solution)/shard_map/ppermute | solution.py:17
  43.6 6.5 %collective-permute-start.6 = (f32[1,2,4,64]{3,2,1,0:T(4,128)S(1)}, f32[1,2,4,64]{3,2,1,0:T(4,128)S(1)}, u32[]{:S(2)}, u32[]{:S(2)}) collective-permute-start(f32[1,2,4,64]{3,2,1,0:T(4,128)S(1)} %get-tuple-element.79), channel_id=1, source_target_pairs={{0,8},{8,16},{16,24},{24,0},{1,9},{9,17},{17,25},{25,1},{2,10},{10... | collective-permute-start | bytes 6152 | tf_op jit(solution)/shard_map/ppermute | solution.py:17
  43.6 8.0 %collective-permute-start.7 = (f32[1,2,4,64]{3,2,1,0:T(4,128)S(1)}, f32[1,2,4,64]{3,2,1,0:T(4,128)S(1)}, u32[]{:S(2)}, u32[]{:S(2)}) collective-permute-start(f32[1,2,4,64]{3,2,1,0:T(4,128)S(1)} %get-tuple-element.79), channel_id=1, source_target_pairs={{8,0},{16,8},{24,16},{0,24},{9,1},{17,9},{25,17},{1,25},{10,2},{18... | collective-permute-start | bytes 6152 | tf_op jit(solution)/shard_map/ppermute | solution.py:19
  61.4 6.5 %collective-permute-start.10 = (f32[1,2,4,64]{3,2,1,0:T(4,128)S(1)}, f32[1,2,4,64]{3,2,1,0:T(4,128)S(1)}, u32[]{:S(2)}, u32[]{:S(2)}) collective-permute-start(f32[1,2,4,64]{3,2,1,0:T(4,128)S(1)} %get-tuple-element.75), channel_id=1, source_target_pairs={{0,8},{8,16},{16,24},{24,0},{1,9},{9,17},{17,25},{25,1},{2,10},{10... | collective-permute-start | bytes 6152 | tf_op jit(solution)/shard_map/ppermute | solution.py:17
  61.5 8.0 %collective-permute-start.11 = (f32[1,2,4,64]{3,2,1,0:T(4,128)S(1)}, f32[1,2,4,64]{3,2,1,0:T(4,128)S(1)}, u32[]{:S(2)}, u32[]{:S(2)}) collective-permute-start(f32[1,2,4,64]{3,2,1,0:T(4,128)S(1)} %get-tuple-element.75), channel_id=1, source_target_pairs={{8,0},{16,8},{24,16},{0,24},{9,1},{17,9},{25,17},{1,25},{10,2},{18... | collective-permute-start | bytes 6152 | tf_op jit(solution)/shard_map/ppermute | solution.py:19
  79.6 6.5 %collective-permute-start.14 = (f32[1,2,4,64]{3,2,1,0:T(4,128)S(1)}, f32[1,2,4,64]{3,2,1,0:T(4,128)S(1)}, u32[]{:S(2)}, u32[]{:S(2)}) collective-permute-start(f32[1,2,4,64]{3,2,1,0:T(4,128)S(1)} %get-tuple-element.71), channel_id=1, source_target_pairs={{0,8},{8,16},{16,24},{24,0},{1,9},{9,17},{17,25},{25,1},{2,10},{10... | collective-permute-start | bytes 6152 | tf_op jit(solution)/shard_map/ppermute | solution.py:17
  79.6 8.0 %collective-permute-start.15 = (f32[1,2,4,64]{3,2,1,0:T(4,128)S(1)}, f32[1,2,4,64]{3,2,1,0:T(4,128)S(1)}, u32[]{:S(2)}, u32[]{:S(2)}) collective-permute-start(f32[1,2,4,64]{3,2,1,0:T(4,128)S(1)} %get-tuple-element.71), channel_id=1, source_target_pairs={{8,0},{16,8},{24,16},{0,24},{9,1},{17,9},{25,17},{1,25},{10,2},{18... | collective-permute-start | bytes 6152 | tf_op jit(solution)/shard_map/ppermute | solution.py:19
  97.4 6.5 %collective-permute-start.18 = (f32[1,2,4,64]{3,2,1,0:T(4,128)S(1)}, f32[1,2,4,64]{3,2,1,0:T(4,128)S(1)}, u32[]{:S(2)}, u32[]{:S(2)}) collective-permute-start(f32[1,2,4,64]{3,2,1,0:T(4,128)S(1)} %get-tuple-element.67), channel_id=1, source_target_pairs={{0,8},{8,16},{16,24},{24,0},{1,9},{9,17},{17,25},{25,1},{2,10},{10... | collective-permute-start | bytes 6152 | tf_op jit(solution)/shard_map/ppermute | solution.py:17
  97.4 8.0 %collective-permute-start.19 = (f32[1,2,4,64]{3,2,1,0:T(4,128)S(1)}, f32[1,2,4,64]{3,2,1,0:T(4,128)S(1)}, u32[]{:S(2)}, u32[]{:S(2)}) collective-permute-start(f32[1,2,4,64]{3,2,1,0:T(4,128)S(1)} %get-tuple-element.67), channel_id=1, source_target_pairs={{8,0},{16,8},{24,16},{0,24},{9,1},{17,9},{25,17},{1,25},{10,2},{18... | collective-permute-start | bytes 6152 | tf_op jit(solution)/shard_map/ppermute | solution.py:19
  99.2 6.3 %collective-permute-start.16 = (f32[1,1,4,64]{3,2,1,0:T(4,128)S(1)}, f32[1,1,4,64]{3,2,1,0:T(4,128)S(1)}, u32[]{:S(2)}, u32[]{:S(2)}) collective-permute-start(f32[1,1,4,64]{3,2,1,0:T(4,128)S(1)} %get-tuple-element.69), channel_id=1, source_target_pairs={{0,1},{1,2},{2,3},{3,4},{4,5},{5,6},{6,7},{7,0},{8,9},{9,10},{10,1... | collective-permute-start | bytes 3080 | tf_op jit(solution)/shard_map/ppermute | solution.py:17
  136.8 6.5 %collective-permute-start.22 = (f32[1,2,4,64]{3,2,1,0:T(4,128)S(1)}, f32[1,2,4,64]{3,2,1,0:T(4,128)S(1)}, u32[]{:S(2)}, u32[]{:S(2)}) collective-permute-start(f32[1,2,4,64]{3,2,1,0:T(4,128)S(1)} %get-tuple-element.63), channel_id=1, source_target_pairs={{0,8},{8,16},{16,24},{24,0},{1,9},{9,17},{17,25},{25,1},{2,10},{10... | collective-permute-start | bytes 6152 | tf_op jit(solution)/shard_map/ppermute | solution.py:17
  136.8 8.0 %collective-permute-start.23 = (f32[1,2,4,64]{3,2,1,0:T(4,128)S(1)}, f32[1,2,4,64]{3,2,1,0:T(4,128)S(1)}, u32[]{:S(2)}, u32[]{:S(2)}) collective-permute-start(f32[1,2,4,64]{3,2,1,0:T(4,128)S(1)} %get-tuple-element.63), channel_id=1, source_target_pairs={{8,0},{16,8},{24,16},{0,24},{9,1},{17,9},{25,17},{1,25},{10,2},{18... | collective-permute-start | bytes 6152 | tf_op jit(solution)/shard_map/ppermute | solution.py:19
  138.6 6.3 %collective-permute-start.20 = (f32[1,1,4,64]{3,2,1,0:T(4,128)S(1)}, f32[1,1,4,64]{3,2,1,0:T(4,128)S(1)}, u32[]{:S(2)}, u32[]{:S(2)}) collective-permute-start(f32[1,1,4,64]{3,2,1,0:T(4,128)S(1)} %get-tuple-element.65), channel_id=1, source_target_pairs={{0,1},{1,2},{2,3},{3,4},{4,5},{5,6},{6,7},{7,0},{8,9},{9,10},{10,1... | collective-permute-start | bytes 3080 | tf_op jit(solution)/shard_map/ppermute | solution.py:17
  182.3 6.5 %collective-permute-start.26 = (f32[1,2,4,64]{3,2,1,0:T(4,128)S(1)}, f32[1,2,4,64]{3,2,1,0:T(4,128)S(1)}, u32[]{:S(2)}, u32[]{:S(2)}) collective-permute-start(f32[1,2,4,64]{3,2,1,0:T(4,128)S(1)} %get-tuple-element.59), channel_id=1, source_target_pairs={{0,8},{8,16},{16,24},{24,0},{1,9},{9,17},{17,25},{25,1},{2,10},{10... | collective-permute-start | bytes 6152 | tf_op jit(solution)/shard_map/ppermute | solution.py:17
  182.3 8.0 %collective-permute-start.27 = (f32[1,2,4,64]{3,2,1,0:T(4,128)S(1)}, f32[1,2,4,64]{3,2,1,0:T(4,128)S(1)}, u32[]{:S(2)}, u32[]{:S(2)}) collective-permute-start(f32[1,2,4,64]{3,2,1,0:T(4,128)S(1)} %get-tuple-element.59), channel_id=1, source_target_pairs={{8,0},{16,8},{24,16},{0,24},{9,1},{17,9},{25,17},{1,25},{10,2},{18... | collective-permute-start | bytes 6152 | tf_op jit(solution)/shard_map/ppermute | solution.py:19
  184.1 6.3 %collective-permute-start.24 = (f32[1,1,4,64]{3,2,1,0:T(4,128)S(1)}, f32[1,1,4,64]{3,2,1,0:T(4,128)S(1)}, u32[]{:S(2)}, u32[]{:S(2)}) collective-permute-start(f32[1,1,4,64]{3,2,1,0:T(4,128)S(1)} %get-tuple-element.61), channel_id=1, source_target_pairs={{0,1},{1,2},{2,3},{3,4},{4,5},{5,6},{6,7},{7,0},{8,9},{9,10},{10,1... | collective-permute-start | bytes 3080 | tf_op jit(solution)/shard_map/ppermute | solution.py:17
  200.5 6.5 %collective-permute-start.30 = (f32[1,2,4,64]{3,2,1,0:T(4,128)S(1)}, f32[1,2,4,64]{3,2,1,0:T(4,128)S(1)}, u32[]{:S(2)}, u32[]{:S(2)}) collective-permute-start(f32[1,2,4,64]{3,2,1,0:T(4,128)S(1)} %get-tuple-element.55), channel_id=1, source_target_pairs={{0,8},{8,16},{16,24},{24,0},{1,9},{9,17},{17,25},{25,1},{2,10},{10... | collective-permute-start | bytes 6152 | tf_op jit(solution)/shard_map/ppermute | solution.py:17
  200.5 8.0 %collective-permute-start.31 = (f32[1,2,4,64]{3,2,1,0:T(4,128)S(1)}, f32[1,2,4,64]{3,2,1,0:T(4,128)S(1)}, u32[]{:S(2)}, u32[]{:S(2)}) collective-permute-start(f32[1,2,4,64]{3,2,1,0:T(4,128)S(1)} %get-tuple-element.55), channel_id=1, source_target_pairs={{8,0},{16,8},{24,16},{0,24},{9,1},{17,9},{25,17},{1,25},{10,2},{18... | collective-permute-start | bytes 6152 | tf_op jit(solution)/shard_map/ppermute | solution.py:19
  218.3 6.5 %collective-permute-start.34 = (f32[1,2,4,64]{3,2,1,0:T(4,128)S(1)}, f32[1,2,4,64]{3,2,1,0:T(4,128)S(1)}, u32[]{:S(2)}, u32[]{:S(2)}) collective-permute-start(f32[1,2,4,64]{3,2,1,0:T(4,128)S(1)} %get-tuple-element.51), channel_id=1, source_target_pairs={{0,8},{8,16},{16,24},{24,0},{1,9},{9,17},{17,25},{25,1},{2,10},{10... | collective-permute-start | bytes 6152 | tf_op jit(solution)/shard_map/ppermute | solution.py:17
  218.3 8.0 %collective-permute-start.35 = (f32[1,2,4,64]{3,2,1,0:T(4,128)S(1)}, f32[1,2,4,64]{3,2,1,0:T(4,128)S(1)}, u32[]{:S(2)}, u32[]{:S(2)}) collective-permute-start(f32[1,2,4,64]{3,2,1,0:T(4,128)S(1)} %get-tuple-element.51), channel_id=1, source_target_pairs={{8,0},{16,8},{24,16},{0,24},{9,1},{17,9},{25,17},{1,25},{10,2},{18... | collective-permute-start | bytes 6152 | tf_op jit(solution)/shard_map/ppermute | solution.py:19
  257.7 6.5 %collective-permute-start.38 = (f32[1,2,4,64]{3,2,1,0:T(4,128)S(1)}, f32[1,2,4,64]{3,2,1,0:T(4,128)S(1)}, u32[]{:S(2)}, u32[]{:S(2)}) collective-permute-start(f32[1,2,4,64]{3,2,1,0:T(4,128)S(1)} %get-tuple-element.47), channel_id=1, source_target_pairs={{0,8},{8,16},{16,24},{24,0},{1,9},{9,17},{17,25},{25,1},{2,10},{10... | collective-permute-start | bytes 6152 | tf_op jit(solution)/shard_map/ppermute | solution.py:17
  257.7 8.0 %collective-permute-start.39 = (f32[1,2,4,64]{3,2,1,0:T(4,128)S(1)}, f32[1,2,4,64]{3,2,1,0:T(4,128)S(1)}, u32[]{:S(2)}, u32[]{:S(2)}) collective-permute-start(f32[1,2,4,64]{3,2,1,0:T(4,128)S(1)} %get-tuple-element.47), channel_id=1, source_target_pairs={{8,0},{16,8},{24,16},{0,24},{9,1},{17,9},{25,17},{1,25},{10,2},{18... | collective-permute-start | bytes 6152 | tf_op jit(solution)/shard_map/ppermute | solution.py:19
  303.2 6.5 %collective-permute-start.42 = (f32[1,2,4,64]{3,2,1,0:T(4,128)S(1)}, f32[1,2,4,64]{3,2,1,0:T(4,128)S(1)}, u32[]{:S(2)}, u32[]{:S(2)}) collective-permute-start(f32[1,2,4,64]{3,2,1,0:T(4,128)S(1)} %get-tuple-element.43), channel_id=1, source_target_pairs={{0,8},{8,16},{16,24},{24,0},{1,9},{9,17},{17,25},{25,1},{2,10},{10... | collective-permute-start | bytes 6152 | tf_op jit(solution)/shard_map/ppermute | solution.py:17
  303.2 8.0 %collective-permute-start.43 = (f32[1,2,4,64]{3,2,1,0:T(4,128)S(1)}, f32[1,2,4,64]{3,2,1,0:T(4,128)S(1)}, u32[]{:S(2)}, u32[]{:S(2)}) collective-permute-start(f32[1,2,4,64]{3,2,1,0:T(4,128)S(1)} %get-tuple-element.43), channel_id=1, source_target_pairs={{8,0},{16,8},{24,16},{0,24},{9,1},{17,9},{25,17},{1,25},{10,2},{18... | collective-permute-start | bytes 6152 | tf_op jit(solution)/shard_map/ppermute | solution.py:19
  321.3 6.5 %collective-permute-start.46 = (f32[1,2,4,64]{3,2,1,0:T(4,128)S(1)}, f32[1,2,4,64]{3,2,1,0:T(4,128)S(1)}, u32[]{:S(2)}, u32[]{:S(2)}) collective-permute-start(f32[1,2,4,64]{3,2,1,0:T(4,128)S(1)} %get-tuple-element.39), channel_id=1, source_target_pairs={{0,8},{8,16},{16,24},{24,0},{1,9},{9,17},{17,25},{25,1},{2,10},{10... | collective-permute-start | bytes 6152 | tf_op jit(solution)/shard_map/ppermute | solution.py:17
  321.4 8.0 %collective-permute-start.47 = (f32[1,2,4,64]{3,2,1,0:T(4,128)S(1)}, f32[1,2,4,64]{3,2,1,0:T(4,128)S(1)}, u32[]{:S(2)}, u32[]{:S(2)}) collective-permute-start(f32[1,2,4,64]{3,2,1,0:T(4,128)S(1)} %get-tuple-element.39), channel_id=1, source_target_pairs={{8,0},{16,8},{24,16},{0,24},{9,1},{17,9},{25,17},{1,25},{10,2},{18... | collective-permute-start | bytes 6152 | tf_op jit(solution)/shard_map/ppermute | solution.py:19
  339.2 6.5 %collective-permute-start.50 = (f32[1,2,4,64]{3,2,1,0:T(4,128)S(1)}, f32[1,2,4,64]{3,2,1,0:T(4,128)S(1)}, u32[]{:S(2)}, u32[]{:S(2)}) collective-permute-start(f32[1,2,4,64]{3,2,1,0:T(4,128)S(1)} %get-tuple-element.35), channel_id=1, source_target_pairs={{0,8},{8,16},{16,24},{24,0},{1,9},{9,17},{17,25},{25,1},{2,10},{10... | collective-permute-start | bytes 6152 | tf_op jit(solution)/shard_map/ppermute | solution.py:17
  339.2 8.0 %collective-permute-start.51 = (f32[1,2,4,64]{3,2,1,0:T(4,128)S(1)}, f32[1,2,4,64]{3,2,1,0:T(4,128)S(1)}, u32[]{:S(2)}, u32[]{:S(2)}) collective-permute-start(f32[1,2,4,64]{3,2,1,0:T(4,128)S(1)} %get-tuple-element.35), channel_id=1, source_target_pairs={{8,0},{16,8},{24,16},{0,24},{9,1},{17,9},{25,17},{1,25},{10,2},{18... | collective-permute-start | bytes 6152 | tf_op jit(solution)/shard_map/ppermute | solution.py:19
  378.6 6.5 %collective-permute-start.54 = (f32[1,2,4,64]{3,2,1,0:T(4,128)S(1)}, f32[1,2,4,64]{3,2,1,0:T(4,128)S(1)}, u32[]{:S(2)}, u32[]{:S(2)}) collective-permute-start(f32[1,2,4,64]{3,2,1,0:T(4,128)S(1)} %get-tuple-element.31), channel_id=1, source_target_pairs={{0,8},{8,16},{16,24},{24,0},{1,9},{9,17},{17,25},{25,1},{2,10},{10... | collective-permute-start | bytes 6152 | tf_op jit(solution)/shard_map/ppermute | solution.py:17
  378.6 8.0 %collective-permute-start.55 = (f32[1,2,4,64]{3,2,1,0:T(4,128)S(1)}, f32[1,2,4,64]{3,2,1,0:T(4,128)S(1)}, u32[]{:S(2)}, u32[]{:S(2)}) collective-permute-start(f32[1,2,4,64]{3,2,1,0:T(4,128)S(1)} %get-tuple-element.31), channel_id=1, source_target_pairs={{8,0},{16,8},{24,16},{0,24},{9,1},{17,9},{25,17},{1,25},{10,2},{18... | collective-permute-start | bytes 6152 | tf_op jit(solution)/shard_map/ppermute | solution.py:19
  (30 other events, 209.1 us)
